TPU v7x, 32 devices: a whole 2x2x4 slice. The times are simulated.
32 devices in a mesh: gx: 4 (over y, x), gy: 4 (over z), gz: 2 (over core).
Axes of the slice: x: 2, y: 2, z: 4, core: 2. Of those that a mesh axis runs over, the one named last changes fastest.
Arguments:
- load: float32 [256, 256, 256], P('gx', 'gy', 'gz'), may hold values from -12 to 12
- stiffness: float32 [256, 256, 256], P('gx', 'gy', 'gz'), may hold values from 0.02 to 2
- prestress: float32 [256, 256], P(('gx', 'gy'), 'gz'), may hold values from -3 to 3
- state_var: float32 [256, 256], P(('gx', 'gy'), 'gz'), may hold values from -1 to 1
- normal_a: float32 [256, 256], P(('gx', 'gy'), 'gz'), may hold values from 1 to 3
Outputs:
- displacement: float32 [256, 256, 256], P('gx', 'gy', 'gz')
- slip_rate: float32 [256, 256], P(('gx', 'gy'), 'gz')
All inputs are finite; a program needn't handle non-finite values.
Results may differ from a plain program's by a relative error of at most 0.0003.
Values sent between devices are 32-bit elements; how exact they have to be, the bound alone decides.
A program may use at most 128 MiB of HBM per device.

v0:
```python
import jax
import jax.numpy as jnp
from jax import lax
from jax.sharding import PartitionSpec as P

ITERS = 3


def extended(cells, sides, width):
    for axis, dim in sides:
        count = lax.axis_size(axis)
        ends = count - 1
        head = lax.slice_in_dim(cells, 0, width, axis=dim)
        tail = lax.slice_in_dim(cells, cells.shape[dim] - width, cells.shape[dim], axis=dim)
        cells = jnp.concatenate(
            [
                lax.ppermute(tail, axis, [(i, (i + 1) % count) for i in range(ends)]),
                cells,
                lax.ppermute(head, axis, [((i + 1) % count, i) for i in range(ends)]),
            ],
            axis=dim,
        )
    return cells


def shifted(padded, sizes_now, axis_num, offset):
    slicers = [slice(2, 2 + sizes_now[0]), slice(2, 2 + sizes_now[1]), slice(2, 2 + sizes_now[2])]
    slicers[axis_num] = slice(2 + offset, 2 + offset + sizes_now[axis_num])
    return padded[tuple(slicers)]


def operate(field, stiffness):
    padded = extended(field, (("gx", 0), ("gy", 1), ("gz", 2)), 2)
    sizes_now = field.shape
    near_sum = jnp.zeros_like(field)
    for axis_num in range(3):
        near_sum = near_sum + 16.0 * (
            shifted(padded, sizes_now, axis_num, 1) + shifted(padded, sizes_now, axis_num, -1)
        )
        near_sum = near_sum - (
            shifted(padded, sizes_now, axis_num, 2) + shifted(padded, sizes_now, axis_num, -2)
        )
    return (7.5 + stiffness) * field - near_sum / 12.0


def paired_sums(residual, precond, image):
    return lax.psum((jnp.sum(residual * precond), jnp.sum(image * precond)), ("gx", "gy", "gz"))


def per_device(load, stiffness, prestress, state_var, normal_a):
    inverse = 1.0 / (7.5 + stiffness)
    solution = jnp.zeros_like(load)
    residual = load
    precond = inverse * residual
    image = operate(precond, stiffness)
    gamma, delta = paired_sums(residual, precond, image)
    alpha = gamma / delta
    direction = precond
    along = image
    for iteration in range(ITERS):
        solution = solution + alpha * direction
        residual = residual - alpha * along
        if iteration + 1 < ITERS:
            precond = inverse * residual
            image = operate(precond, stiffness)
            gamma_new, delta = paired_sums(residual, precond, image)
            ratio = gamma_new / gamma
            alpha = gamma_new / (delta - ratio * gamma_new / alpha)
            direction = precond + ratio * direction
            along = image + ratio * along
            gamma = gamma_new
    rows_y = solution.shape[1]
    total_y = rows_y * lax.axis_size("gy")
    edge_rows = jnp.concatenate((solution[:, :2, :], solution[:, rows_y - 2 :, :]), axis=1)
    local_rows = jnp.array([0, 1, rows_y - 2, rows_y - 1], dtype=jnp.int32)
    global_y = lax.axis_index("gy") * rows_y + local_rows
    offset = global_y - (total_y // 2 - 2)
    weights = (
        (offset == 0).astype(jnp.float32)
        - 27.0 * (offset == 1).astype(jnp.float32)
        + 27.0 * (offset == 2).astype(jnp.float32)
        - (offset == 3).astype(jnp.float32)
    ) / 24.0
    fault_term = jnp.sum(edge_rows * weights[None, :, None], axis=1)
    owned_rows = solution.shape[0] // lax.axis_size("gy")
    whole_strip = lax.psum(fault_term, "gy")
    traction = lax.dynamic_slice_in_dim(
        whole_strip, lax.axis_index("gy") * owned_rows, owned_rows, 0
    )
    slip_rate = jnp.exp(-state_var) * jnp.sinh((prestress + 2.0 * traction) / normal_a)
    return (solution, slip_rate)


def solution(mesh):
    placed = (
        P("gx", "gy", "gz"),
        P("gx", "gy", "gz"),
        P(("gx", "gy"), "gz"),
        P(("gx", "gy"), "gz"),
        P(("gx", "gy"), "gz"),
    )
    return jax.shard_map(
        per_device,
        mesh=mesh,
        in_specs=placed,
        out_specs=(P("gx", "gy", "gz"), P(("gx", "gy"), "gz")),
        check_vma=False,
    )
```

profile of v0, /device:TPU:0, one launch (start us, length us, event | category | flops | bytes accessed | tf_op | source)
XLA Modules:
  0.0 352.4 jit_solution(6903636222099214039)
XLA Ops:
  0.6 4.7 %copy_multiply_fusion = f32[64,64,128]{2,0,1:T(8,128)S(1)} fusion(f32[64,64,128]{2,1,0:T(8,128)} %param.6, f32[64,64,128]{2,1,0:T(8,128)} %param.7), kind=kLoop, calls=%fused_computation.122 | loop fusion | flops 1572864 | bytes 6291456 | tf_op jit(solution)/shard_map/mul | solution.py:54
  5.3 1.3 collective-permute-start
  6.6 5.5 %collective-permute-start.1 = (f32[2,64,128]{2,0,1:T(2,128)S(1)}, f32[2,64,128]{2,0,1:T(2,128)S(1)}, u32[]{:S(2)}, u32[]{:S(2)}) collective-permute-start(f32[2,64,128]{2,0,1:T(2,128)S(1)} %get-tuple-element.48), channel_id=1, source_target_pairs={{0,8},{8,16},{16,24},{1,9},{9,17},{17,25},{2,10},{10,18},{18,26},{... | collective-permute-start | bytes 196616 | tf_op jit(solution)/shard_map/ppermute | solution.py:17
  12.5 1.6 collective-permute-done.1
  15.4 4.6 %collective-permute-start.3 = (f32[68,2,128]{2,0,1:T(8,128)S(1)}, f32[68,2,128]{2,0,1:T(8,128)S(1)}, u32[]{:S(2)}, u32[]{:S(2)}) collective-permute-start(f32[68,2,128]{2,0,1:T(8,128)S(1)} %get-tuple-element.40), channel_id=1, source_target_pairs={{0,2},{2,4},{4,6},{1,3},{3,5},{5,7},{8,10},{10,12},{12,14},{9,11},... | collective-permute-start | bytes 208904 | tf_op jit(solution)/shard_map/ppermute | solution.py:17
  20.4 1.6 collective-permute-done.3
  22.3 3.0 fusion.63
  25.3 2.6 copy.112
  27.9 1.3 collective-permute-start.5
  29.2 2.6 copy.110
  33.1 2.6 pad_maximum_fusion.3
  35.8 2.4 copy.113
  38.2 2.4 copy.111
  40.6 13.9 %multiply_reduce_fusion.3 = (f32[]{:T(128)}, f32[]{:T(128)}, f32[64,64,128]{2,0,1:T(8,128)}) fusion(f32[64,64,128]{2,0,1:T(8,128)S(1)} %copy_multiply_fusion, f32[64,64,128]{2,1,0:T(8,128)} %param.6, f32[68,2,128]{2,0,1:T(8,128)S(1)} %collective-permute-done.2, f32[2,64,128]{2,0,1:T(2,128)S(1)} %collective-permute-done, ...), kind=kLoop, calls=%fused_computation.119 | loop fusion | flops 24117248 | bytes 17121544 | tf_op jit(solution)/shard_map/reduce_sum | solution.py:47
  54.5 44.4 %all-reduce.2 = (f32[]{:T(128)}, f32[]{:T(128)}) all-reduce(f32[]{:T(128)} %get-tuple-element.13, f32[]{:T(128)} %get-tuple-element.12), channel_id=1, replica_groups=mesh['gx'=4,'gy'=4,'gz'=2] {'gx','gy','gz'}, use_global_device_ids=true, to_apply=%region_1.0 | all-reduce | flops 2 | bytes 16 | tf_op jit(solution)/shard_map/psum | solution.py:47
  100.3 5.3 %fusion.48 = f32[64,64,128]{2,0,1:T(8,128)S(1)} fusion(f32[64,64,128]{2,0,1:T(8,128)} %get-tuple-element.23, f32[]{:T(128)S(6)} %div.45, f32[64,64,128]{2,1,0:T(8,128)} %param.6, f32[64,64,128]{2,1,0:T(8,128)} %param.7), kind=kLoop, calls=%fused_computation.124 | loop fusion | flops 2621440 | bytes 8388612 | tf_op jit(solution)/shard_map/mul | solution.py:64
  107.0 4.8 %collective-permute-start.7 = (f32[2,64,128]{2,0,1:T(2,128)S(1)}, f32[2,64,128]{2,0,1:T(2,128)S(1)}, u32[]{:S(2)}, u32[]{:S(2)}) collective-permute-start(f32[2,64,128]{2,0,1:T(2,128)S(1)} %get-tuple-element.46), channel_id=1, source_target_pairs={{0,8},{8,16},{16,24},{1,9},{9,17},{17,25},{2,10},{10,18},{18,26},{... | collective-permute-start | bytes 196616 | tf_op jit(solution)/shard_map/ppermute | solution.py:17
  112.1 1.6 collective-permute-done.7
  115.0 4.5 %collective-permute-start.9 = (f32[68,2,128]{2,0,1:T(8,128)S(1)}, f32[68,2,128]{2,0,1:T(8,128)S(1)}, u32[]{:S(2)}, u32[]{:S(2)}) collective-permute-start(f32[68,2,128]{2,0,1:T(8,128)S(1)} %get-tuple-element.36), channel_id=1, source_target_pairs={{0,2},{2,4},{4,6},{1,3},{3,5},{5,7},{8,10},{10,12},{12,14},{9,11},... | collective-permute-start | bytes 208904 | tf_op jit(solution)/shard_map/ppermute | solution.py:17
  120.0 1.6 collective-permute-done.9
  121.9 3.0 fusion.62
  124.9 2.6 copy.117
  127.5 1.3 collective-permute-start.11
  128.8 2.6 copy.115
  132.7 5.0 %pad_maximum_fusion.4 = (f32[68,66,128]{2,0,1:T(8,128)}, f32[68,66,128]{2,0,1:T(8,128)}) fusion(f32[68,2,128]{2,0,1:T(8,128)S(1)} %collective-permute-done.8, f32[2,64,128]{2,0,1:T(2,128)S(1)} %collective-permute-done.6, f32[64,64,128]{2,0,1:T(8,128)} %copy-done.1, f32[2,64,128]{2,0,1:T(2,128)S(1)} %collective-permute-done.7, ...), kind=kLoop, calls=%fused_computation.5 | loop fusion | flops 3446784 | bytes 6963200 | tf_op jit(solution)/shard_map/concatenate | solution.py:15
  137.7 2.4 copy.118
  140.1 2.4 copy.116
  142.5 22.0 %multiply_reduce_fusion.1 = (f32[]{:T(128)}, f32[]{:T(128)}, f32[64,64,128]{2,0,1:T(8,128)}) fusion(f32[64,64,128]{2,0,1:T(8,128)} %copy-done.1, f32[64,64,128]{2,0,1:T(8,128)} %get-tuple-element.23, f32[]{:T(128)S(6)} %div.45, f32[64,64,128]{2,1,0:T(8,128)} %param.6, f32[68,2,128]{2,0,1:T(8,128)S(1)} %collective-permute-done.8, ...), kind=kLoop, calls=%fused_computation.116 | loop fusion | flops 25165824 | bytes 19218700 | tf_op jit(solution)/shard_map/reduce_sum | solution.py:47
  164.5 44.4 %all-reduce.1 = (f32[]{:T(128)}, f32[]{:T(128)}) all-reduce(f32[]{:T(128)} %get-tuple-element.11, f32[]{:T(128)} %get-tuple-element.10), channel_id=1, replica_groups=mesh['gx'=4,'gy'=4,'gz'=2] {'gx','gy','gz'}, use_global_device_ids=true, to_apply=%region_5.0 | all-reduce | flops 2 | bytes 16 | tf_op jit(solution)/shard_map/psum | solution.py:47
  213.5 6.6 %multiply_reduce_fusion = (f32[]{:T(128)}, f32[64,64,128]{2,0,1:T(8,128)S(1)}) fusion(f32[64,64,128]{2,1,0:T(8,128)} %param.7, f32[64,64,128]{2,0,1:T(8,128)} %get-tuple-element.22, f32[64,64,128]{2,0,1:T(8,128)} %get-tuple-element.23, f32[]{:T(128)S(6)} %div.47, f32[]{:T(128)S(6)} %div.49, f32[]{:T(128)S(6)} %div.45, f32[64,64,128]{2,1,0:T(8,128)} %param.6), kind=kLoop, calls=%fused_computation.114 | loop fusion | flops 5767167 | bytes 10485776 | tf_op jit(solution)/shard_map/reduce_sum | solution.py:47
  220.1 1.3 copy-done
  222.8 4.8 %collective-permute-start.13 = (f32[2,64,128]{2,0,1:T(2,128)S(1)}, f32[2,64,128]{2,0,1:T(2,128)S(1)}, u32[]{:S(2)}, u32[]{:S(2)}) collective-permute-start(f32[2,64,128]{2,0,1:T(2,128)S(1)} %get-tuple-element.44), channel_id=1, source_target_pairs={{0,8},{8,16},{16,24},{1,9},{9,17},{17,25},{2,10},{10,18},{18,26},{... | collective-permute-start | bytes 196616 | tf_op jit(solution)/shard_map/ppermute | solution.py:17
  227.9 1.6 collective-permute-done.13
  231.7 4.5 %collective-permute-start.15 = (f32[68,2,128]{2,0,1:T(8,128)S(1)}, f32[68,2,128]{2,0,1:T(8,128)S(1)}, u32[]{:S(2)}, u32[]{:S(2)}) collective-permute-start(f32[68,2,128]{2,0,1:T(8,128)S(1)} %get-tuple-element.32), channel_id=1, source_target_pairs={{0,2},{2,4},{4,6},{1,3},{3,5},{5,7},{8,10},{10,12},{12,14},{9,11},... | collective-permute-start | bytes 208904 | tf_op jit(solution)/shard_map/ppermute | solution.py:17
  236.7 1.6 collective-permute-done.15
  238.2 1.8 pad_maximum_fusion.2
  240.1 3.0 fusion.61
  243.1 2.6 copy.121
  245.7 1.3 collective-permute-start.17
  247.0 2.6 copy.119
  250.9 5.0 %pad_maximum_fusion.5 = (f32[68,66,128]{2,0,1:T(8,128)}, f32[68,66,128]{2,0,1:T(8,128)}) fusion(f32[68,2,128]{2,0,1:T(8,128)S(1)} %collective-permute-done.14, f32[2,64,128]{2,0,1:T(2,128)S(1)} %collective-permute-done.12, f32[64,64,128]{2,0,1:T(8,128)} %copy-done, f32[2,64,128]{2,0,1:T(2,128)S(1)} %collective-permute-done.13, ...), kind=kLoop, calls=%fused_computation.7 | loop fusion | flops 3446784 | bytes 6963200 | tf_op jit(solution)/shard_map/concatenate | solution.py:15
  255.9 2.4 copy.122
  258.3 2.4 copy.120
  260.7 19.1 %fusion.46 = f32[]{:T(128)} fusion(f32[64,64,128]{2,0,1:T(8,128)} %copy-done, f32[68,2,128]{2,0,1:T(8,128)S(1)} %collective-permute-done.14, f32[2,64,128]{2,0,1:T(2,128)S(1)} %collective-permute-done.12, f32[2,64,128]{2,0,1:T(2,128)S(1)} %collective-permute-done.13, f32[68,2,128]{2,0,1:T(8,128)S(1)} %collective-permute-done.15, f32[68,68,2]{2,0,1:T(8,128)} %copy.122, ...), kind=kLoop, calls=%fused_computation.121 | loop fusion | flops 23068672 | bytes 12927236 | tf_op jit(solution)/shard_map/reduce_sum | solution.py:47
  279.8 44.4 %all-reduce = (f32[]{:T(128)}, f32[]{:T(128)}) all-reduce(f32[]{:T(128)} %get-tuple-element.20, f32[]{:T(128)} %fusion.46), channel_id=1, replica_groups=mesh['gx'=4,'gy'=4,'gz'=2] {'gx','gy','gz'}, use_global_device_ids=true, to_apply=%region_9.0 | all-reduce | flops 2 | bytes 16 | tf_op jit(solution)/shard_map/psum | solution.py:47
  328.1 3.0 multiply_add_fusion
  331.1 2.5 copy.125
  333.8 17.9 %psum.55 = f32[64,128]{1,0:T(8,128)S(1)} all-reduce(f32[64,128]{1,0:T(8,128)S(1)} %fusion.49), channel_id=1, replica_groups=mesh['gx'=4,'gy'=4,'gz'=2] {'gy'}, use_global_device_ids=true, to_apply=%region_13.0 | all-reduce | flops 8192 | bytes 65536 | tf_op jit(solution)/shard_map/psum | solution.py:86
  (43 shorter events, 14.9 us)
Async XLA Ops:
  5.3 7.1 %collective-permute-start = (f32[2,64,128]{2,0,1:T(2,128)S(1)}, f32[2,64,128]{2,0,1:T(2,128)S(1)}, u32[]{:S(2)}, u32[]{:S(2)}) collective-permute-start(f32[2,64,128]{2,0,1:T(2,128)S(1)} %get-tuple-element.49), channel_id=1, source_target_pairs={{8,0},{16,8},{24,16},{9,1},{17,9},{25,17},{10,2},{18,10},{26,18},{... | collective-permute-start | bytes 196616 | tf_op jit(solution)/shard_map/ppermute | solution.py:19
  6.6 7.4 %collective-permute-start.1 = (f32[2,64,128]{2,0,1:T(2,128)S(1)}, f32[2,64,128]{2,0,1:T(2,128)S(1)}, u32[]{:S(2)}, u32[]{:S(2)}) collective-permute-start(f32[2,64,128]{2,0,1:T(2,128)S(1)} %get-tuple-element.48), channel_id=1, source_target_pairs={{0,8},{8,16},{16,24},{1,9},{9,17},{17,25},{2,10},{10,18},{18,26},{... | collective-permute-start | bytes 196616 | tf_op jit(solution)/shard_map/ppermute | solution.py:17
  14.1 6.3 %collective-permute-start.2 = (f32[68,2,128]{2,0,1:T(8,128)S(1)}, f32[68,2,128]{2,0,1:T(8,128)S(1)}, u32[]{:S(2)}, u32[]{:S(2)}) collective-permute-start(f32[68,2,128]{2,0,1:T(8,128)S(1)} %get-tuple-element.41), channel_id=1, source_target_pairs={{2,0},{4,2},{6,4},{3,1},{5,3},{7,5},{10,8},{12,10},{14,12},{11,9},... | collective-permute-start | bytes 208904 | tf_op jit(solution)/shard_map/ppermute | solution.py:19
  15.4 6.6 %collective-permute-start.3 = (f32[68,2,128]{2,0,1:T(8,128)S(1)}, f32[68,2,128]{2,0,1:T(8,128)S(1)}, u32[]{:S(2)}, u32[]{:S(2)}) collective-permute-start(f32[68,2,128]{2,0,1:T(8,128)S(1)} %get-tuple-element.40), channel_id=1, source_target_pairs={{0,2},{2,4},{4,6},{1,3},{3,5},{5,7},{8,10},{10,12},{12,14},{9,11},... | collective-permute-start | bytes 208904 | tf_op jit(solution)/shard_map/ppermute | solution.py:17
  27.9 7.8 %collective-permute-start.5 = (f32[68,68,2]{1,0,2:T(8,128)S(1)}, f32[68,68,2]{1,0,2:T(8,128)S(1)}, u32[]{:S(2)}, u32[]{:S(2)}) collective-permute-start(f32[68,68,2]{1,0,2:T(8,128)S(1)} %copy.112), channel_id=1, source_target_pairs={{0,1},{2,3},{4,5},{6,7},{8,9},{10,11},{12,13},{14,15},{16,17},{18,... | collective-permute-start | bytes 110984 | tf_op jit(solution)/shard_map/ppermute | solution.py:17
  31.8 6.3 %collective-permute-start.4 = (f32[68,68,2]{1,0,2:T(8,128)S(1)}, f32[68,68,2]{1,0,2:T(8,128)S(1)}, u32[]{:S(2)}, u32[]{:S(2)}) collective-permute-start(f32[68,68,2]{1,0,2:T(8,128)S(1)} %copy.110), channel_id=1, source_target_pairs={{1,0},{3,2},{5,4},{7,6},{9,8},{11,10},{13,12},{15,14},{17,16},{19,... | collective-permute-start | bytes 110984 | tf_op jit(solution)/shard_map/ppermute | solution.py:19
  105.6 15.9 %copy-start.1 = (f32[64,64,128]{2,0,1:T(8,128)}, f32[64,64,128]{2,0,1:T(8,128)S(1)}, u32[]{:S(2)}) copy-start(f32[64,64,128]{2,0,1:T(8,128)S(1)} %fusion.48) | copy-start | bytes 6291460
  105.7 6.4 %collective-permute-start.6 = (f32[2,64,128]{2,0,1:T(2,128)S(1)}, f32[2,64,128]{2,0,1:T(2,128)S(1)}, u32[]{:S(2)}, u32[]{:S(2)}) collective-permute-start(f32[2,64,128]{2,0,1:T(2,128)S(1)} %get-tuple-element.47), channel_id=1, source_target_pairs={{8,0},{16,8},{24,16},{9,1},{17,9},{25,17},{10,2},{18,10},{26,18},{... | collective-permute-start | bytes 196616 | tf_op jit(solution)/shard_map/ppermute | solution.py:19
  107.0 6.7 %collective-permute-start.7 = (f32[2,64,128]{2,0,1:T(2,128)S(1)}, f32[2,64,128]{2,0,1:T(2,128)S(1)}, u32[]{:S(2)}, u32[]{:S(2)}) collective-permute-start(f32[2,64,128]{2,0,1:T(2,128)S(1)} %get-tuple-element.46), channel_id=1, source_target_pairs={{0,8},{8,16},{16,24},{1,9},{9,17},{17,25},{2,10},{10,18},{18,26},{... | collective-permute-start | bytes 196616 | tf_op jit(solution)/shard_map/ppermute | solution.py:17
  113.7 6.2 %collective-permute-start.8 = (f32[68,2,128]{2,0,1:T(8,128)S(1)}, f32[68,2,128]{2,0,1:T(8,128)S(1)}, u32[]{:S(2)}, u32[]{:S(2)}) collective-permute-start(f32[68,2,128]{2,0,1:T(8,128)S(1)} %get-tuple-element.37), channel_id=1, source_target_pairs={{2,0},{4,2},{6,4},{3,1},{5,3},{7,5},{10,8},{12,10},{14,12},{11,9},... | collective-permute-start | bytes 208904 | tf_op jit(solution)/shard_map/ppermute | solution.py:19
  115.0 6.5 %collective-permute-start.9 = (f32[68,2,128]{2,0,1:T(8,128)S(1)}, f32[68,2,128]{2,0,1:T(8,128)S(1)}, u32[]{:S(2)}, u32[]{:S(2)}) collective-permute-start(f32[68,2,128]{2,0,1:T(8,128)S(1)} %get-tuple-element.36), channel_id=1, source_target_pairs={{0,2},{2,4},{4,6},{1,3},{3,5},{5,7},{8,10},{10,12},{12,14},{9,11},... | collective-permute-start | bytes 208904 | tf_op jit(solution)/shard_map/ppermute | solution.py:17
  127.5 10.2 %collective-permute-start.11 = (f32[68,68,2]{1,0,2:T(8,128)S(1)}, f32[68,68,2]{1,0,2:T(8,128)S(1)}, u32[]{:S(2)}, u32[]{:S(2)}) collective-permute-start(f32[68,68,2]{1,0,2:T(8,128)S(1)} %copy.117), channel_id=1, source_target_pairs={{0,1},{2,3},{4,5},{6,7},{8,9},{10,11},{12,13},{14,15},{16,17},{18,... | collective-permute-start | bytes 110984 | tf_op jit(solution)/shard_map/ppermute | solution.py:17
  131.4 8.7 %collective-permute-start.10 = (f32[68,68,2]{1,0,2:T(8,128)S(1)}, f32[68,68,2]{1,0,2:T(8,128)S(1)}, u32[]{:S(2)}, u32[]{:S(2)}) collective-permute-start(f32[68,68,2]{1,0,2:T(8,128)S(1)} %copy.115), channel_id=1, source_target_pairs={{1,0},{3,2},{5,4},{7,6},{9,8},{11,10},{13,12},{15,14},{17,16},{19,... | collective-permute-start | bytes 110984 | tf_op jit(solution)/shard_map/ppermute | solution.py:19
  220.1 1.3 copy-start
  220.1 16.1 %copy-start.5 = (s32[4]{0:T(128)S(1)}, s32[4]{0:T(128)}, u32[]{:S(2)}) copy-start(s32[4]{0:T(128)} %constant.51.clone) | copy-start | bytes 52
  221.5 6.4 %collective-permute-start.12 = (f32[2,64,128]{2,0,1:T(2,128)S(1)}, f32[2,64,128]{2,0,1:T(2,128)S(1)}, u32[]{:S(2)}, u32[]{:S(2)}) collective-permute-start(f32[2,64,128]{2,0,1:T(2,128)S(1)} %get-tuple-element.45), channel_id=1, source_target_pairs={{8,0},{16,8},{24,16},{9,1},{17,9},{25,17},{10,2},{18,10},{26,18},{... | collective-permute-start | bytes 196616 | tf_op jit(solution)/shard_map/ppermute | solution.py:19
  222.8 6.7 %collective-permute-start.13 = (f32[2,64,128]{2,0,1:T(2,128)S(1)}, f32[2,64,128]{2,0,1:T(2,128)S(1)}, u32[]{:S(2)}, u32[]{:S(2)}) collective-permute-start(f32[2,64,128]{2,0,1:T(2,128)S(1)} %get-tuple-element.44), channel_id=1, source_target_pairs={{0,8},{8,16},{16,24},{1,9},{9,17},{17,25},{2,10},{10,18},{18,26},{... | collective-permute-start | bytes 196616 | tf_op jit(solution)/shard_map/ppermute | solution.py:17
  230.4 6.2 %collective-permute-start.14 = (f32[68,2,128]{2,0,1:T(8,128)S(1)}, f32[68,2,128]{2,0,1:T(8,128)S(1)}, u32[]{:S(2)}, u32[]{:S(2)}) collective-permute-start(f32[68,2,128]{2,0,1:T(8,128)S(1)} %get-tuple-element.33), channel_id=1, source_target_pairs={{2,0},{4,2},{6,4},{3,1},{5,3},{7,5},{10,8},{12,10},{14,12},{11,9},... | collective-permute-start | bytes 208904 | tf_op jit(solution)/shard_map/ppermute | solution.py:19
  231.7 6.5 %collective-permute-start.15 = (f32[68,2,128]{2,0,1:T(8,128)S(1)}, f32[68,2,128]{2,0,1:T(8,128)S(1)}, u32[]{:S(2)}, u32[]{:S(2)}) collective-permute-start(f32[68,2,128]{2,0,1:T(8,128)S(1)} %get-tuple-element.32), channel_id=1, source_target_pairs={{0,2},{2,4},{4,6},{1,3},{3,5},{5,7},{8,10},{10,12},{12,14},{9,11},... | collective-permute-start | bytes 208904 | tf_op jit(solution)/shard_map/ppermute | solution.py:17
  245.7 10.2 %collective-permute-start.17 = (f32[68,68,2]{1,0,2:T(8,128)S(1)}, f32[68,68,2]{1,0,2:T(8,128)S(1)}, u32[]{:S(2)}, u32[]{:S(2)}) collective-permute-start(f32[68,68,2]{1,0,2:T(8,128)S(1)} %copy.121), channel_id=1, source_target_pairs={{0,1},{2,3},{4,5},{6,7},{8,9},{10,11},{12,13},{14,15},{16,17},{18,... | collective-permute-start | bytes 110984 | tf_op jit(solution)/shard_map/ppermute | solution.py:17
  249.6 8.7 %collective-permute-start.16 = (f32[68,68,2]{1,0,2:T(8,128)S(1)}, f32[68,68,2]{1,0,2:T(8,128)S(1)}, u32[]{:S(2)}, u32[]{:S(2)}) collective-permute-start(f32[68,68,2]{1,0,2:T(8,128)S(1)} %copy.119), channel_id=1, source_target_pairs={{1,0},{3,2},{5,4},{7,6},{9,8},{11,10},{13,12},{15,14},{17,16},{19,... | collective-permute-start | bytes 110984 | tf_op jit(solution)/shard_map/ppermute | solution.py:19
  331.1 20.6 %copy-start.2 = (f32[16,128]{1,0:T(8,128)S(1)}, f32[16,128]{1,0:T(8,128)}, u32[]{:S(2)}) copy-start(f32[16,128]{1,0:T(8,128)} %param.10) | copy-start | bytes 24580
  331.1 20.6 %copy-start.3 = (f32[16,128]{1,0:T(8,128)S(1)}, f32[16,128]{1,0:T(8,128)}, u32[]{:S(2)}) copy-start(f32[16,128]{1,0:T(8,128)} %param.8) | copy-start | bytes 24580
  331.1 20.6 %copy-start.4 = (f32[16,128]{1,0:T(8,128)S(1)}, f32[16,128]{1,0:T(8,128)}, u32[]{:S(2)}) copy-start(f32[16,128]{1,0:T(8,128)} %param.9) | copy-start | bytes 24580
where the time goes:
time: 354 us; the launch traced here: 352 us
  blocking collectives  151 us (43%)
  other arithmetic  91.3 us (26%)
  starting transfers between devices  44.4 us (13%)
  local copies, waits for them, and re-layouts  43.1 us (12%)
  waiting for transfers between devices  11.5 us (3%)
  between operations  10.9 us (3%)
    psum x3, blocking collectives, paired_sums(): lax.psum((jnp.sum(residual * precond), jnp.sum(image * precond)), ('gx',...  133 us
    reduce_sum x3, other arithmetic, paired_sums(): jnp.sum(image * precond)  55 us
    ppermute x9, starting transfers between devices, extended(): lax.ppermute(tail, axis, [(i, (i + 1) % count) for i in range(ends)])  32.7 us
    psum x1, blocking collectives, per_device(): whole_strip = lax.psum(fault_term, 'gy')  17.9 us
    slice x6, local copies, waits for them, and re-layouts, extended(): head = lax.slice_in_dim(cells, 0, width, axis=dim)  16.8 us
    concatenate x9, other arithmetic, extended(): jnp.concatenate([lax.ppermute(tail, axis, [(i, (i + 1) % count) for i in...  16 us
    ppermute x9, starting transfers between devices, extended(): lax.ppermute(head, axis, [((i + 1) % count, i) for i in range(ends)])  11.6 us
    mul x2, other arithmetic, per_device(): precond = inverse * residual  9.98 us
  transfers between devices with their start and end apart: 18, of which 12 were waited for; matrix products, arithmetic and copies ran while one was open for 8% of the time, Pallas kernels for 0%

commit v1 on v0

--- a/solution.py
+++ b/solution.py
@@ -44,7 +44,9 @@
 
 
 def paired_sums(residual, precond, image):
-    return lax.psum((jnp.sum(residual * precond), jnp.sum(image * precond)), ("gx", "gy", "gz"))
+    return lax.psum(
+        lax.psum((jnp.sum(residual * precond), jnp.sum(image * precond)), ("gy", "gz")), "gx"
+    )
 
 
 def per_device(load, stiffness, prestress, state_var, normal_a):

time: 354 us -> 303 us (0.86)
  blocking collectives: 151 us -> 102 us
    psum x3 -> x6, blocking collectives: 133 us -> 85.9 us  [the longest x3 51.8 us: paired_sums(): lax.psum((jnp.sum(residual * precond), jnp.sum(image * precond)), ('gy',...]
  transfers between devices with their start and end apart: 18 -> 18, of which waited for: 12 -> 12; matrix products, arithmetic and copies ran while one was open for 8% -> 9% of each run, Pallas kernels for 0% -> 0%
where the time goes in v1:
time: 303 us; the launch traced here: 302 us
  blocking collectives  102 us (34%)
  other arithmetic  91.2 us (30%)
  starting transfers between devices  43.8 us (14%)
  local copies, waits for them, and re-layouts  43.1 us (14%)
  waiting for transfers between devices  11.5 us (4%)
  between operations  10.4 us (3%)
    reduce_sum x3, other arithmetic, paired_sums(): jnp.sum(image * precond)  54.8 us
    psum x3, blocking collectives, paired_sums(): lax.psum((jnp.sum(residual * precond), jnp.sum(image * precond)), ('gy',...  51.8 us
    psum x3, blocking collectives, paired_sums(): lax.psum(lax.psum((jnp.sum(residual * precond), jnp.sum(image * precond))...  34.1 us
    ppermute x9, starting transfers between devices, extended(): lax.ppermute(tail, axis, [(i, (i + 1) % count) for i in range(ends)])  32.2 us
    slice x6, local copies, waits for them, and re-layouts, extended(): head = lax.slice_in_dim(cells, 0, width, axis=dim)  16.8 us
    concatenate x9, other arithmetic, extended(): jnp.concatenate([lax.ppermute(tail, axis, [(i, (i + 1) % count) for i in...  16 us
    psum x1, blocking collectives, per_device(): whole_strip = lax.psum(fault_term, 'gy')  15.8 us
    ppermute x9, starting transfers between devices, extended(): lax.ppermute(head, axis, [((i + 1) % count, i) for i in range(ends)])  11.6 us
  transfers between devices with their start and end apart: 18, of which 12 were waited for; matrix products, arithmetic and copies ran while one was open for 9% of the time, Pallas kernels for 0%

profile of v1, /device:TPU:0, one launch (start us, length us, event | category | flops | bytes accessed | tf_op | source)
XLA Modules:
  0.0 301.7 jit_solution(16403050823120880474)
XLA Ops:
  0.6 4.7 %copy_multiply_fusion = f32[64,64,128]{2,0,1:T(8,128)S(1)} fusion(f32[64,64,128]{2,1,0:T(8,128)} %param.6, f32[64,64,128]{2,1,0:T(8,128)} %param.7), kind=kLoop, calls=%fused_computation.122 | loop fusion | flops 1572864 | bytes 6291456 | tf_op jit(solution)/shard_map/mul | solution.py:56
  6.6 5.5 %collective-permute-start.1 = (f32[2,64,128]{2,0,1:T(2,128)S(1)}, f32[2,64,128]{2,0,1:T(2,128)S(1)}, u32[]{:S(2)}, u32[]{:S(2)}) collective-permute-start(f32[2,64,128]{2,0,1:T(2,128)S(1)} %get-tuple-element.54), channel_id=1, source_target_pairs={{0,8},{8,16},{16,24},{1,9},{9,17},{17,25},{2,10},{10,18},{18,26},{... | collective-permute-start | bytes 196616 | tf_op jit(solution)/shard_map/ppermute | solution.py:17
  12.5 1.6 collective-permute-done.1
  15.4 4.6 %collective-permute-start.3 = (f32[68,2,128]{2,0,1:T(8,128)S(1)}, f32[68,2,128]{2,0,1:T(8,128)S(1)}, u32[]{:S(2)}, u32[]{:S(2)}) collective-permute-start(f32[68,2,128]{2,0,1:T(8,128)S(1)} %get-tuple-element.46), channel_id=1, source_target_pairs={{0,2},{2,4},{4,6},{1,3},{3,5},{5,7},{8,10},{10,12},{12,14},{9,11},... | collective-permute-start | bytes 208904 | tf_op jit(solution)/shard_map/ppermute | solution.py:17
  20.4 1.6 collective-permute-done.3
  22.3 3.0 fusion.63
  25.3 2.6 copy.112
  27.9 1.3 collective-permute-start.5
  29.2 2.6 copy.110
  33.1 2.6 pad_maximum_fusion.3
  35.8 2.4 copy.113
  38.2 2.4 copy.111
  40.6 13.8 %multiply_reduce_fusion.3 = (f32[]{:T(128)}, f32[]{:T(128)}, f32[64,64,128]{2,0,1:T(8,128)}) fusion(f32[64,64,128]{2,0,1:T(8,128)S(1)} %copy_multiply_fusion, f32[64,64,128]{2,1,0:T(8,128)} %param.6, f32[68,2,128]{2,0,1:T(8,128)S(1)} %collective-permute-done.2, f32[2,64,128]{2,0,1:T(2,128)S(1)} %collective-permute-done, ...), kind=kLoop, calls=%fused_computation.119 | loop fusion | flops 24117248 | bytes 17121544 | tf_op jit(solution)/shard_map/reduce_sum | solution.py:48
  54.4 19.8 %all-reduce.2 = (f32[]{:T(128)}, f32[]{:T(128)}) all-reduce(f32[]{:T(128)} %get-tuple-element.13, f32[]{:T(128)} %get-tuple-element.12), channel_id=1, replica_groups=mesh['gx'=4,'gy'=4,'gz'=2] {'gy','gz'}, use_global_device_ids=true, to_apply=%region_1.0 | all-reduce | flops 2 | bytes 16 | tf_op jit(solution)/shard_map/psum | solution.py:48
  74.2 11.6 %all-reduce.5 = (f32[]{:T(128)}, f32[]{:T(128)}) all-reduce(f32[]{:T(128)} %get-tuple-element.18, f32[]{:T(128)} %get-tuple-element.19), channel_id=1, replica_groups=mesh['gx'=4,'gy'=4,'gz'=2] {'gx'}, use_global_device_ids=true, to_apply=%region_2.0 | all-reduce | flops 2 | bytes 16 | tf_op jit(solution)/shard_map/psum | solution.py:47
  87.2 5.3 %fusion.48 = f32[64,64,128]{2,0,1:T(8,128)S(1)} fusion(f32[64,64,128]{2,0,1:T(8,128)} %get-tuple-element.29, f32[]{:T(128)S(6)} %div.45, f32[64,64,128]{2,1,0:T(8,128)} %param.6, f32[64,64,128]{2,1,0:T(8,128)} %param.7), kind=kLoop, calls=%fused_computation.124 | loop fusion | flops 2621440 | bytes 8388612 | tf_op jit(solution)/shard_map/mul | solution.py:66
  93.9 4.5 %collective-permute-start.7 = (f32[2,64,128]{2,0,1:T(2,128)S(1)}, f32[2,64,128]{2,0,1:T(2,128)S(1)}, u32[]{:S(2)}, u32[]{:S(2)}) collective-permute-start(f32[2,64,128]{2,0,1:T(2,128)S(1)} %get-tuple-element.52), channel_id=1, source_target_pairs={{0,8},{8,16},{16,24},{1,9},{9,17},{17,25},{2,10},{10,18},{18,26},{... | collective-permute-start | bytes 196616 | tf_op jit(solution)/shard_map/ppermute | solution.py:17
  98.7 1.6 collective-permute-done.7
  101.6 4.5 %collective-permute-start.9 = (f32[68,2,128]{2,0,1:T(8,128)S(1)}, f32[68,2,128]{2,0,1:T(8,128)S(1)}, u32[]{:S(2)}, u32[]{:S(2)}) collective-permute-start(f32[68,2,128]{2,0,1:T(8,128)S(1)} %get-tuple-element.42), channel_id=1, source_target_pairs={{0,2},{2,4},{4,6},{1,3},{3,5},{5,7},{8,10},{10,12},{12,14},{9,11},... | collective-permute-start | bytes 208904 | tf_op jit(solution)/shard_map/ppermute | solution.py:17
  106.6 1.6 collective-permute-done.9
  108.5 3.0 fusion.62
  111.5 2.6 copy.117
  114.1 1.3 collective-permute-start.11
  115.4 2.6 copy.115
  119.3 5.0 %pad_maximum_fusion.4 = (f32[68,66,128]{2,0,1:T(8,128)}, f32[68,66,128]{2,0,1:T(8,128)}) fusion(f32[68,2,128]{2,0,1:T(8,128)S(1)} %collective-permute-done.8, f32[2,64,128]{2,0,1:T(2,128)S(1)} %collective-permute-done.6, f32[64,64,128]{2,0,1:T(8,128)} %copy-done.1, f32[2,64,128]{2,0,1:T(2,128)S(1)} %collective-permute-done.7, ...), kind=kLoop, calls=%fused_computation.5 | loop fusion | flops 3446784 | bytes 6963200 | tf_op jit(solution)/shard_map/concatenate | solution.py:15
  124.3 2.4 copy.118
  126.7 2.4 copy.116
  129.1 22.1 %multiply_reduce_fusion.1 = (f32[]{:T(128)}, f32[]{:T(128)}, f32[64,64,128]{2,0,1:T(8,128)}) fusion(f32[64,64,128]{2,0,1:T(8,128)} %copy-done.1, f32[64,64,128]{2,0,1:T(8,128)} %get-tuple-element.29, f32[]{:T(128)S(6)} %div.45, f32[64,64,128]{2,1,0:T(8,128)} %param.6, f32[68,2,128]{2,0,1:T(8,128)S(1)} %collective-permute-done.8, ...), kind=kLoop, calls=%fused_computation.116 | loop fusion | flops 25165824 | bytes 19218700 | tf_op jit(solution)/shard_map/reduce_sum | solution.py:48
  151.2 15.3 %all-reduce.1 = (f32[]{:T(128)}, f32[]{:T(128)}) all-reduce(f32[]{:T(128)} %get-tuple-element.11, f32[]{:T(128)} %get-tuple-element.10), channel_id=1, replica_groups=mesh['gx'=4,'gy'=4,'gz'=2] {'gy','gz'}, use_global_device_ids=true, to_apply=%region_7.0 | all-reduce | flops 2 | bytes 16 | tf_op jit(solution)/shard_map/psum | solution.py:48
  166.5 11.1 %all-reduce.4 = (f32[]{:T(128)}, f32[]{:T(128)}) all-reduce(f32[]{:T(128)} %get-tuple-element.16, f32[]{:T(128)} %get-tuple-element.17), channel_id=1, replica_groups=mesh['gx'=4,'gy'=4,'gz'=2] {'gx'}, use_global_device_ids=true, to_apply=%region_8.0 | all-reduce | flops 2 | bytes 16 | tf_op jit(solution)/shard_map/psum | solution.py:47
  181.9 6.6 %multiply_reduce_fusion = (f32[]{:T(128)}, f32[64,64,128]{2,0,1:T(8,128)S(1)}) fusion(f32[64,64,128]{2,1,0:T(8,128)} %param.7, f32[64,64,128]{2,0,1:T(8,128)} %get-tuple-element.28, f32[64,64,128]{2,0,1:T(8,128)} %get-tuple-element.29, f32[]{:T(128)S(6)} %div.47, f32[]{:T(128)S(6)} %div.49, f32[]{:T(128)S(6)} %div.45, f32[64,64,128]{2,1,0:T(8,128)} %param.6), kind=kLoop, calls=%fused_computation.114 | loop fusion | flops 5767167 | bytes 10485776 | tf_op jit(solution)/shard_map/reduce_sum | solution.py:48
  188.5 1.3 copy-done
  191.2 4.6 %collective-permute-start.13 = (f32[2,64,128]{2,0,1:T(2,128)S(1)}, f32[2,64,128]{2,0,1:T(2,128)S(1)}, u32[]{:S(2)}, u32[]{:S(2)}) collective-permute-start(f32[2,64,128]{2,0,1:T(2,128)S(1)} %get-tuple-element.50), channel_id=1, source_target_pairs={{0,8},{8,16},{16,24},{1,9},{9,17},{17,25},{2,10},{10,18},{18,26},{... | collective-permute-start | bytes 196616 | tf_op jit(solution)/shard_map/ppermute | solution.py:17
  199.8 4.5 %collective-permute-start.15 = (f32[68,2,128]{2,0,1:T(8,128)S(1)}, f32[68,2,128]{2,0,1:T(8,128)S(1)}, u32[]{:S(2)}, u32[]{:S(2)}) collective-permute-start(f32[68,2,128]{2,0,1:T(8,128)S(1)} %get-tuple-element.38), channel_id=1, source_target_pairs={{0,2},{2,4},{4,6},{1,3},{3,5},{5,7},{8,10},{10,12},{12,14},{9,11},... | collective-permute-start | bytes 208904 | tf_op jit(solution)/shard_map/ppermute | solution.py:17
  204.7 1.6 collective-permute-done.15
  206.3 1.8 pad_maximum_fusion.2
  208.2 3.0 fusion.61
  211.2 2.6 copy.121
  215.1 2.6 copy.119
  219.0 5.0 %pad_maximum_fusion.5 = (f32[68,66,128]{2,0,1:T(8,128)}, f32[68,66,128]{2,0,1:T(8,128)}) fusion(f32[68,2,128]{2,0,1:T(8,128)S(1)} %collective-permute-done.14, f32[2,64,128]{2,0,1:T(2,128)S(1)} %collective-permute-done.12, f32[64,64,128]{2,0,1:T(8,128)} %copy-done, f32[2,64,128]{2,0,1:T(2,128)S(1)} %collective-permute-done.13, ...), kind=kLoop, calls=%fused_computation.7 | loop fusion | flops 3446784 | bytes 6963200 | tf_op jit(solution)/shard_map/concatenate | solution.py:15
  223.9 2.4 copy.122
  226.3 2.4 copy.120
  228.7 19.0 %fusion.46 = f32[]{:T(128)} fusion(f32[64,64,128]{2,0,1:T(8,128)} %copy-done, f32[68,2,128]{2,0,1:T(8,128)S(1)} %collective-permute-done.14, f32[2,64,128]{2,0,1:T(2,128)S(1)} %collective-permute-done.12, f32[2,64,128]{2,0,1:T(2,128)S(1)} %collective-permute-done.13, f32[68,2,128]{2,0,1:T(8,128)S(1)} %collective-permute-done.15, f32[68,68,2]{2,0,1:T(8,128)} %copy.122, ...), kind=kLoop, calls=%fused_computation.121 | loop fusion | flops 23068672 | bytes 12927236 | tf_op jit(solution)/shard_map/reduce_sum | solution.py:48
  247.7 16.6 %all-reduce = (f32[]{:T(128)}, f32[]{:T(128)}) all-reduce(f32[]{:T(128)} %get-tuple-element.26, f32[]{:T(128)} %fusion.46), channel_id=1, replica_groups=mesh['gx'=4,'gy'=4,'gz'=2] {'gy','gz'}, use_global_device_ids=true, to_apply=%region_13.0 | all-reduce | flops 2 | bytes 16 | tf_op jit(solution)/shard_map/psum | solution.py:48
  264.4 11.4 %all-reduce.3 = (f32[]{:T(128)}, f32[]{:T(128)}) all-reduce(f32[]{:T(128)} %get-tuple-element.14, f32[]{:T(128)} %get-tuple-element.15), channel_id=1, replica_groups=mesh['gx'=4,'gy'=4,'gz'=2] {'gx'}, use_global_device_ids=true, to_apply=%region_14.0 | all-reduce | flops 2 | bytes 16 | tf_op jit(solution)/shard_map/psum | solution.py:47
  279.6 3.0 multiply_add_fusion
  282.6 2.5 copy.125
  285.3 15.8 %psum.103 = f32[64,128]{1,0:T(8,128)S(1)} all-reduce(f32[64,128]{1,0:T(8,128)S(1)} %fusion.49), channel_id=1, replica_groups=mesh['gx'=4,'gy'=4,'gz'=2] {'gy'}, use_global_device_ids=true, to_apply=%region_19.0 | all-reduce | flops 8192 | bytes 65536 | tf_op jit(solution)/shard_map/psum | solution.py:88
  (46 shorter events, 19.1 us)
Async XLA Ops:
  5.3 7.1 %collective-permute-start = (f32[2,64,128]{2,0,1:T(2,128)S(1)}, f32[2,64,128]{2,0,1:T(2,128)S(1)}, u32[]{:S(2)}, u32[]{:S(2)}) collective-permute-start(f32[2,64,128]{2,0,1:T(2,128)S(1)} %get-tuple-element.55), channel_id=1, source_target_pairs={{8,0},{16,8},{24,16},{9,1},{17,9},{25,17},{10,2},{18,10},{26,18},{... | collective-permute-start | bytes 196616 | tf_op jit(solution)/shard_map/ppermute | solution.py:19
  6.6 7.4 %collective-permute-start.1 = (f32[2,64,128]{2,0,1:T(2,128)S(1)}, f32[2,64,128]{2,0,1:T(2,128)S(1)}, u32[]{:S(2)}, u32[]{:S(2)}) collective-permute-start(f32[2,64,128]{2,0,1:T(2,128)S(1)} %get-tuple-element.54), channel_id=1, source_target_pairs={{0,8},{8,16},{16,24},{1,9},{9,17},{17,25},{2,10},{10,18},{18,26},{... | collective-permute-start | bytes 196616 | tf_op jit(solution)/shard_map/ppermute | solution.py:17
  14.1 6.3 %collective-permute-start.2 = (f32[68,2,128]{2,0,1:T(8,128)S(1)}, f32[68,2,128]{2,0,1:T(8,128)S(1)}, u32[]{:S(2)}, u32[]{:S(2)}) collective-permute-start(f32[68,2,128]{2,0,1:T(8,128)S(1)} %get-tuple-element.47), channel_id=1, source_target_pairs={{2,0},{4,2},{6,4},{3,1},{5,3},{7,5},{10,8},{12,10},{14,12},{11,9},... | collective-permute-start | bytes 208904 | tf_op jit(solution)/shard_map/ppermute | solution.py:19
  15.4 6.6 %collective-permute-start.3 = (f32[68,2,128]{2,0,1:T(8,128)S(1)}, f32[68,2,128]{2,0,1:T(8,128)S(1)}, u32[]{:S(2)}, u32[]{:S(2)}) collective-permute-start(f32[68,2,128]{2,0,1:T(8,128)S(1)} %get-tuple-element.46), channel_id=1, source_target_pairs={{0,2},{2,4},{4,6},{1,3},{3,5},{5,7},{8,10},{10,12},{12,14},{9,11},... | collective-permute-start | bytes 208904 | tf_op jit(solution)/shard_map/ppermute | solution.py:17
  27.9 7.8 %collective-permute-start.5 = (f32[68,68,2]{1,0,2:T(8,128)S(1)}, f32[68,68,2]{1,0,2:T(8,128)S(1)}, u32[]{:S(2)}, u32[]{:S(2)}) collective-permute-start(f32[68,68,2]{1,0,2:T(8,128)S(1)} %copy.112), channel_id=1, source_target_pairs={{0,1},{2,3},{4,5},{6,7},{8,9},{10,11},{12,13},{14,15},{16,17},{18,... | collective-permute-start | bytes 110984 | tf_op jit(solution)/shard_map/ppermute | solution.py:17
  31.8 6.3 %collective-permute-start.4 = (f32[68,68,2]{1,0,2:T(8,128)S(1)}, f32[68,68,2]{1,0,2:T(8,128)S(1)}, u32[]{:S(2)}, u32[]{:S(2)}) collective-permute-start(f32[68,68,2]{1,0,2:T(8,128)S(1)} %copy.110), channel_id=1, source_target_pairs={{1,0},{3,2},{5,4},{7,6},{9,8},{11,10},{13,12},{15,14},{17,16},{19,... | collective-permute-start | bytes 110984 | tf_op jit(solution)/shard_map/ppermute | solution.py:19
  92.5 15.7 %copy-start.1 = (f32[64,64,128]{2,0,1:T(8,128)}, f32[64,64,128]{2,0,1:T(8,128)S(1)}, u32[]{:S(2)}) copy-start(f32[64,64,128]{2,0,1:T(8,128)S(1)} %fusion.48) | copy-start | bytes 6291460
  92.6 6.2 %collective-permute-start.6 = (f32[2,64,128]{2,0,1:T(2,128)S(1)}, f32[2,64,128]{2,0,1:T(2,128)S(1)}, u32[]{:S(2)}, u32[]{:S(2)}) collective-permute-start(f32[2,64,128]{2,0,1:T(2,128)S(1)} %get-tuple-element.53), channel_id=1, source_target_pairs={{8,0},{16,8},{24,16},{9,1},{17,9},{25,17},{10,2},{18,10},{26,18},{... | collective-permute-start | bytes 196616 | tf_op jit(solution)/shard_map/ppermute | solution.py:19
  93.9 6.4 %collective-permute-start.7 = (f32[2,64,128]{2,0,1:T(2,128)S(1)}, f32[2,64,128]{2,0,1:T(2,128)S(1)}, u32[]{:S(2)}, u32[]{:S(2)}) collective-permute-start(f32[2,64,128]{2,0,1:T(2,128)S(1)} %get-tuple-element.52), channel_id=1, source_target_pairs={{0,8},{8,16},{16,24},{1,9},{9,17},{17,25},{2,10},{10,18},{18,26},{... | collective-permute-start | bytes 196616 | tf_op jit(solution)/shard_map/ppermute | solution.py:17
  100.3 6.2 %collective-permute-start.8 = (f32[68,2,128]{2,0,1:T(8,128)S(1)}, f32[68,2,128]{2,0,1:T(8,128)S(1)}, u32[]{:S(2)}, u32[]{:S(2)}) collective-permute-start(f32[68,2,128]{2,0,1:T(8,128)S(1)} %get-tuple-element.43), channel_id=1, source_target_pairs={{2,0},{4,2},{6,4},{3,1},{5,3},{7,5},{10,8},{12,10},{14,12},{11,9},... | collective-permute-start | bytes 208904 | tf_op jit(solution)/shard_map/ppermute | solution.py:19
  101.6 6.5 %collective-permute-start.9 = (f32[68,2,128]{2,0,1:T(8,128)S(1)}, f32[68,2,128]{2,0,1:T(8,128)S(1)}, u32[]{:S(2)}, u32[]{:S(2)}) collective-permute-start(f32[68,2,128]{2,0,1:T(8,128)S(1)} %get-tuple-element.42), channel_id=1, source_target_pairs={{0,2},{2,4},{4,6},{1,3},{3,5},{5,7},{8,10},{10,12},{12,14},{9,11},... | collective-permute-start | bytes 208904 | tf_op jit(solution)/shard_map/ppermute | solution.py:17
  114.1 10.2 %collective-permute-start.11 = (f32[68,68,2]{1,0,2:T(8,128)S(1)}, f32[68,68,2]{1,0,2:T(8,128)S(1)}, u32[]{:S(2)}, u32[]{:S(2)}) collective-permute-start(f32[68,68,2]{1,0,2:T(8,128)S(1)} %copy.117), channel_id=1, source_target_pairs={{0,1},{2,3},{4,5},{6,7},{8,9},{10,11},{12,13},{14,15},{16,17},{18,... | collective-permute-start | bytes 110984 | tf_op jit(solution)/shard_map/ppermute | solution.py:17
  118.0 8.7 %collective-permute-start.10 = (f32[68,68,2]{1,0,2:T(8,128)S(1)}, f32[68,68,2]{1,0,2:T(8,128)S(1)}, u32[]{:S(2)}, u32[]{:S(2)}) collective-permute-start(f32[68,68,2]{1,0,2:T(8,128)S(1)} %copy.115), channel_id=1, source_target_pairs={{1,0},{3,2},{5,4},{7,6},{9,8},{11,10},{13,12},{15,14},{17,16},{19,... | collective-permute-start | bytes 110984 | tf_op jit(solution)/shard_map/ppermute | solution.py:19
  188.5 1.3 copy-start
  188.5 15.9 %copy-start.5 = (s32[4]{0:T(128)S(1)}, s32[4]{0:T(128)}, u32[]{:S(2)}) copy-start(s32[4]{0:T(128)} %constant.51.clone) | copy-start | bytes 52
  189.9 6.6 %collective-permute-start.12 = (f32[2,64,128]{2,0,1:T(2,128)S(1)}, f32[2,64,128]{2,0,1:T(2,128)S(1)}, u32[]{:S(2)}, u32[]{:S(2)}) collective-permute-start(f32[2,64,128]{2,0,1:T(2,128)S(1)} %get-tuple-element.51), channel_id=1, source_target_pairs={{8,0},{16,8},{24,16},{9,1},{17,9},{25,17},{10,2},{18,10},{26,18},{... | collective-permute-start | bytes 196616 | tf_op jit(solution)/shard_map/ppermute | solution.py:19
  191.2 6.4 %collective-permute-start.13 = (f32[2,64,128]{2,0,1:T(2,128)S(1)}, f32[2,64,128]{2,0,1:T(2,128)S(1)}, u32[]{:S(2)}, u32[]{:S(2)}) collective-permute-start(f32[2,64,128]{2,0,1:T(2,128)S(1)} %get-tuple-element.50), channel_id=1, source_target_pairs={{0,8},{8,16},{16,24},{1,9},{9,17},{17,25},{2,10},{10,18},{18,26},{... | collective-permute-start | bytes 196616 | tf_op jit(solution)/shard_map/ppermute | solution.py:17
  198.5 6.2 %collective-permute-start.14 = (f32[68,2,128]{2,0,1:T(8,128)S(1)}, f32[68,2,128]{2,0,1:T(8,128)S(1)}, u32[]{:S(2)}, u32[]{:S(2)}) collective-permute-start(f32[68,2,128]{2,0,1:T(8,128)S(1)} %get-tuple-element.39), channel_id=1, source_target_pairs={{2,0},{4,2},{6,4},{3,1},{5,3},{7,5},{10,8},{12,10},{14,12},{11,9},... | collective-permute-start | bytes 208904 | tf_op jit(solution)/shard_map/ppermute | solution.py:19
  199.8 6.5 %collective-permute-start.15 = (f32[68,2,128]{2,0,1:T(8,128)S(1)}, f32[68,2,128]{2,0,1:T(8,128)S(1)}, u32[]{:S(2)}, u32[]{:S(2)}) collective-permute-start(f32[68,2,128]{2,0,1:T(8,128)S(1)} %get-tuple-element.38), channel_id=1, source_target_pairs={{0,2},{2,4},{4,6},{1,3},{3,5},{5,7},{8,10},{10,12},{12,14},{9,11},... | collective-permute-start | bytes 208904 | tf_op jit(solution)/shard_map/ppermute | solution.py:17
  213.8 10.2 %collective-permute-start.17 = (f32[68,68,2]{1,0,2:T(8,128)S(1)}, f32[68,68,2]{1,0,2:T(8,128)S(1)}, u32[]{:S(2)}, u32[]{:S(2)}) collective-permute-start(f32[68,68,2]{1,0,2:T(8,128)S(1)} %copy.121), channel_id=1, source_target_pairs={{0,1},{2,3},{4,5},{6,7},{8,9},{10,11},{12,13},{14,15},{16,17},{18,... | collective-permute-start | bytes 110984 | tf_op jit(solution)/shard_map/ppermute | solution.py:17
  217.7 8.7 %collective-permute-start.16 = (f32[68,68,2]{1,0,2:T(8,128)S(1)}, f32[68,68,2]{1,0,2:T(8,128)S(1)}, u32[]{:S(2)}, u32[]{:S(2)}) collective-permute-start(f32[68,68,2]{1,0,2:T(8,128)S(1)} %copy.119), channel_id=1, source_target_pairs={{1,0},{3,2},{5,4},{7,6},{9,8},{11,10},{13,12},{15,14},{17,16},{19,... | collective-permute-start | bytes 110984 | tf_op jit(solution)/shard_map/ppermute | solution.py:19
  282.6 18.4 %copy-start.2 = (f32[16,128]{1,0:T(8,128)S(1)}, f32[16,128]{1,0:T(8,128)}, u32[]{:S(2)}) copy-start(f32[16,128]{1,0:T(8,128)} %param.10) | copy-start | bytes 24580
  282.6 18.4 %copy-start.3 = (f32[16,128]{1,0:T(8,128)S(1)}, f32[16,128]{1,0:T(8,128)}, u32[]{:S(2)}) copy-start(f32[16,128]{1,0:T(8,128)} %param.8) | copy-start | bytes 24580
  282.6 18.4 %copy-start.4 = (f32[16,128]{1,0:T(8,128)S(1)}, f32[16,128]{1,0:T(8,128)}, u32[]{:S(2)}) copy-start(f32[16,128]{1,0:T(8,128)} %param.9) | copy-start | bytes 24580
